TPU v7x, 32 devices: a whole 2x2x4 slice. The times are simulated.
32 devices in a mesh: dp: 8 (over z, y), mp: 4 (over x, core).
Axes of the slice: x: 2, y: 2, z: 4, core: 2. Of those that a mesh axis runs over, the one named last changes fastest.
Arguments:
- tokens: bfloat16 [6144, 768], P(('dp', 'mp')), may hold values from -6 to 6
- obs_mask: int32 [96, 64], P(('dp', 'mp')), may hold values 0 or 1
- norm_gains: float32 [5, 768], replicated, may hold values from 0.1 to 1.9
- attn_in: bfloat16 [2, 3, 768, 768], P(None, None, 'dp', 'mp'), may hold values from -0.21875 to 0.21875
- attn_out: bfloat16 [2, 768, 768], P(None, 'mp', 'dp'), may hold values from -0.21875 to 0.21875
- mlp_in: bfloat16 [2, 768, 3072], P(None, 'dp', 'mp'), may hold values from -0.21875 to 0.21875
- mlp_out: bfloat16 [2, 3072, 768], P(None, 'mp', 'dp'), may hold values from -0.109375 to 0.109375
- embodiment: int32 [96, 1], P('dp'), may hold values from 0 to 24; in each aligned block of 12 rows (0 to 11, 12 to 23, ...) no two rows name the same one
- levels: int32 [96, 2], P('dp'), may hold values from 0 to 19
- actions: bfloat16 [96, 2, 56], P('dp'), may hold values from -1 to 1
- noise: bfloat16 [96, 2, 56], P('dp'), may hold values from -5 to 5
- action_dims: int32 [25], replicated, may hold values from 7 to 14
- head_read: bfloat16 [32, 768, 256], P('dp'), may hold values from -0.21875 to 0.21875
- head_act: bfloat16 [32, 56, 256], P('dp'), may hold values from -0.75 to 0.75
- time_table: bfloat16 [32, 20, 256], P('dp'), may hold values from -5 to 5
- block_in: bfloat16 [32, 256, 256], P('dp'), may hold values from -0.375 to 0.375
- block_out: bfloat16 [32, 256, 256], P('dp'), may hold values from -0.375 to 0.375
- head_out: bfloat16 [32, 256, 56], P('dp'), may hold values from -0.375 to 0.375
Outputs:
- readout_grad: bfloat16 [96, 2, 768], P(('dp', 'mp'))
- grad_read: float32 [32, 768, 256], P('dp', 'mp')
- grad_act: float32 [32, 56, 256], P('dp')
- grad_time: float32 [32, 20, 256], P('dp')
- grad_block_in: float32 [32, 256, 256], P('dp')
- grad_block_out: float32 [32, 256, 256], P('dp')
- grad_head_out: float32 [32, 256, 56], P('dp')
Inputs may be any that keep to these rules, and one draw needn't show every extreme that they name: Within each aligned block of 12 samples (those of one dp index) no embodiment appears twice; every embodiment appears in some block.
All inputs are finite; a program needn't handle non-finite values. No bound on the sum of `obs_mask` on one device may be relied on, other than what follows from the above.
Results may differ from a plain program's by a relative error of at most 0.024.
Values may be sent and summed in bfloat16 or wider, within the bound.
A program may use at most 64 MiB of HBM per device.

v0:
```python
import math
import jax
import jax.numpy as jnp
from jax import lax
from jax.sharding import PartitionSpec as P

D = 768
HDIM = 64
EMB = 25
READ = 2
LEVELS = 20
ADIM_MAX = 14
ACT = 56
norm_eps = 1e-05


def normalize(values, scale_gain):
    center = values - jnp.mean(values, axis=-1, keepdims=True)
    spread = jnp.mean(center * center, axis=-1, keepdims=True)
    return center * lax.rsqrt(spread + norm_eps) * scale_gain


def allowed_keys(observed):
    length = observed.shape[1]
    position = jnp.arange(length)
    visible = (observed == 1) & (position < length - READ)[None, :]
    itself = position[:, None] == position[None, :]
    return visible[:, None, :] | itself[None, :, :]


def attend(queries, key_rows, value_rows, allowed):
    scores = jnp.einsum(
        "sqhd,skhd->shqk", queries, key_rows, preferred_element_type=jnp.float32
    ) * HDIM ** (-0.5)
    weights = jnp.where(allowed[:, None, :, :], jnp.exp(scores), 0.0)
    shares = (weights / jnp.sum(weights, axis=-1, keepdims=True)).astype(jnp.bfloat16)
    context = jnp.einsum("shqk,skhd->sqhd", shares, value_rows, preferred_element_type=jnp.float32)
    return context.astype(jnp.bfloat16)


def plan():
    steps_up = (jnp.arange(LEVELS, dtype=jnp.float32) + 1.0) / LEVELS
    anchor = math.cos(0.008 / 1.008 * math.pi / 2) ** 2
    return jnp.cos((steps_up + 0.008) / 1.008 * (math.pi / 2)) ** 2 / anchor


def noisy_pair(level_ids, clean, noise_draw, table):
    picked = (level_ids[..., None] == jnp.arange(LEVELS)).astype(jnp.float32)
    kept = jnp.sum(picked * table, axis=-1)[..., None]
    mixed = jnp.sqrt(kept) * clean.astype(jnp.float32) + jnp.sqrt(1.0 - kept) * noise_draw.astype(
        jnp.float32
    )
    return mixed.astype(jnp.bfloat16)


def tail(first, target, weight_mask, inner_weight, outer_weight, final_weight):
    highest = lax.Precision.HIGHEST
    active = jax.nn.silu(first).astype(jnp.bfloat16)
    inner = jnp.dot(active, inner_weight, preferred_element_type=jnp.float32, precision=highest)
    second = jax.nn.silu(inner).astype(jnp.bfloat16)
    hidden = first + jnp.dot(
        second, outer_weight, preferred_element_type=jnp.float32, precision=highest
    )
    third = jax.nn.silu(hidden).astype(jnp.bfloat16)
    predicted = jnp.dot(third, final_weight, preferred_element_type=jnp.float32, precision=highest)
    differ = predicted - target
    return 0.5 * jnp.sum(weight_mask * differ * differ)


def gather_rows(normed, observed):
    return (
        lax.all_gather(normed, "mp", axis=0, tiled=True),
        lax.all_gather(observed, "mp", axis=0, tiled=True),
    )


def reduce_rows(partial_value):
    return lax.psum_scatter(
        partial_value.astype(jnp.bfloat16), "mp", scatter_dimension=0, tiled=True
    ).astype(jnp.float32)


def head_grads(first, inner_weight, outer_weight, final_weight, target, weight_mask):

    def head_loss(first_in, inner_in, outer_in, final_in):
        return tail(first_in, target, weight_mask, inner_in, outer_in, final_in)

    loss_value, pullback = jax.vjp(head_loss, first, inner_weight, outer_weight, final_weight)
    return pullback(jnp.ones((), jnp.float32))


def on_device(
    tokens,
    obs_mask,
    norm_gains,
    attn_in,
    attn_out,
    mlp_in,
    mlp_out,
    embodiment,
    levels,
    actions,
    noise,
    action_dims,
    head_read,
    head_act,
    time_table,
    block_in,
    block_out,
    head_out,
):
    group_width = attn_in.shape[3]
    heads_local = group_width // HDIM
    samples_local = obs_mask.shape[0]
    length = obs_mask.shape[1]
    layer_count = attn_in.shape[0]
    residual = tokens.astype(jnp.float32)
    for layer_index in range(layer_count):
        normed = normalize(residual, norm_gains[2 * layer_index]).astype(jnp.bfloat16)
        gathered, mask_group = gather_rows(normed, obs_mask)
        samples_group = mask_group.shape[0]
        columns = gathered
        projected = jnp.einsum(
            "td,jdc->jtc",
            columns,
            lax.all_gather(attn_in[layer_index], "dp", axis=1, tiled=True),
            preferred_element_type=jnp.float32,
        )
        projected = projected.astype(jnp.bfloat16).reshape(
            3, samples_group, length, heads_local, HDIM
        )
        context = attend(
            projected[0], projected[1], projected[2], allowed_keys(mask_group)
        ).reshape(-1, group_width)
        partial_value = jnp.dot(
            context,
            lax.all_gather(attn_out[layer_index], "dp", axis=1, tiled=True),
            preferred_element_type=jnp.float32,
        )
        residual = residual + reduce_rows(partial_value)
        normed = normalize(residual, norm_gains[2 * layer_index + 1]).astype(jnp.bfloat16)
        gathered, mask_group = gather_rows(normed, obs_mask)
        raised = jnp.dot(
            gathered,
            lax.all_gather(mlp_in[layer_index], "dp", axis=0, tiled=True),
            preferred_element_type=jnp.float32,
        )
        hidden = jax.nn.gelu(raised, approximate=True).astype(jnp.bfloat16)
        partial_value = jnp.dot(
            hidden,
            lax.all_gather(mlp_out[layer_index], "dp", axis=1, tiled=True),
            preferred_element_type=jnp.float32,
        )
        residual = residual + reduce_rows(partial_value)
    ending = residual.reshape(samples_local, length, D)[:, length - READ :, :]
    readouts = normalize(ending, norm_gains[2 * layer_count]).astype(jnp.bfloat16)
    table = plan()
    heads_dev = head_read.shape[0]
    peers = lax.axis_size("dp")
    slot_count = heads_dev * peers
    my_model = lax.axis_index("mp")
    my_owner = lax.axis_index("dp")
    features = lax.all_to_all(readouts, "mp", split_axis=2, concat_axis=0, tiled=True)
    owners = embodiment[:, 0]
    feature_width = features.shape[2]
    paired = jnp.concatenate([noisy_pair(levels, actions, noise, table), noise], axis=-1)
    send_features = (
        jnp.zeros((slot_count, READ, feature_width), jnp.bfloat16).at[owners].set(features)
    )
    send_paired = jnp.zeros((slot_count, READ, 2 * ACT), jnp.bfloat16).at[owners].set(paired)
    send_levels = jnp.full((slot_count, READ), -1, jnp.int32).at[owners].set(levels)
    got_features, got_paired, got_levels = (
        lax.all_to_all(
            send_features.reshape(peers, heads_dev * READ, feature_width),
            "dp",
            split_axis=0,
            concat_axis=0,
            tiled=True,
        ),
        lax.all_to_all(
            send_paired.reshape(peers, heads_dev * READ, 2 * ACT),
            "dp",
            split_axis=0,
            concat_axis=0,
            tiled=True,
        ),
        lax.all_to_all(
            send_levels.reshape(peers, heads_dev * READ),
            "dp",
            split_axis=0,
            concat_axis=0,
            tiled=True,
        ),
    )

    def by_head(values):
        trailing = values.shape[2:]
        values = values.reshape((peers, heads_dev, READ) + trailing)
        values = jnp.moveaxis(values, 1, 0)
        return values.reshape((heads_dev, peers * READ) + trailing)

    head_features = by_head(got_features)
    head_paired = by_head(got_paired)
    head_levels = by_head(got_levels)
    head_noisy = head_paired[..., :ACT]
    head_target = head_paired[..., ACT:].astype(jnp.float32)
    head_onehot = (head_levels[..., None] == jnp.arange(LEVELS)).astype(jnp.bfloat16)
    slot_ids = my_owner * heads_dev + jnp.arange(heads_dev)
    dims_here = jnp.sum(
        jnp.where(jnp.arange(EMB)[None, :] == slot_ids[:, None], action_dims[None, :], 0), axis=1
    )
    column = jnp.arange(ACT) % ADIM_MAX
    weight_mask = (head_levels >= 0).astype(jnp.float32)[..., None] * (
        column[None, None, :] < dims_here[:, None, None]
    ).astype(jnp.float32)
    others = jnp.einsum("hna,hac->hnc", head_noisy, head_act, preferred_element_type=jnp.float32)
    others = others + jnp.einsum(
        "hnl,hlc->hnc", head_onehot, time_table, preferred_element_type=jnp.float32
    )
    read_weight = lax.dynamic_slice_in_dim(head_read, my_model * feature_width, feature_width, 1)
    first = (
        lax.psum(
            jnp.einsum(
                "hnd,hdc->hnc", head_features, read_weight, preferred_element_type=jnp.float32
            ).astype(jnp.bfloat16),
            "mp",
        ).astype(jnp.float32)
        + others
    )
    grad_first, grad_inner, grad_outer, grad_final = jax.vmap(head_grads)(
        first,
        block_in.astype(jnp.float32),
        block_out.astype(jnp.float32),
        head_out.astype(jnp.float32),
        head_target,
        weight_mask,
    )
    grad_bf = grad_first.astype(jnp.bfloat16)
    grad_readin = jnp.einsum(
        "hnd,hnc->hdc", head_features, grad_bf, preferred_element_type=jnp.float32
    )
    grad_actin = jnp.einsum("hna,hnc->hac", head_noisy, grad_bf, preferred_element_type=jnp.float32)
    grad_timein = jnp.einsum(
        "hnl,hnc->hlc", head_onehot, grad_bf, preferred_element_type=jnp.float32
    )
    backward = jnp.einsum(
        "hnc,hdc->hnd", grad_bf, read_weight, preferred_element_type=jnp.float32
    ).astype(jnp.bfloat16)
    backward = jnp.moveaxis(backward.reshape(heads_dev, peers, READ, feature_width), 0, 1).reshape(
        peers, heads_dev * READ, feature_width
    )
    arrived = lax.all_to_all(backward, "dp", split_axis=0, concat_axis=0, tiled=True)
    arrived = arrived.reshape(slot_count, READ, feature_width)[owners]
    arrived = lax.all_to_all(arrived, "mp", split_axis=0, concat_axis=2, tiled=True)
    return (arrived, grad_readin, grad_actin, grad_timein, grad_inner, grad_outer, grad_final)


def solution(mesh):
    placed = (
        P(("dp", "mp"), None),
        P(("dp", "mp"), None),
        P(),
        P(None, None, "dp", "mp"),
        P(None, "mp", "dp"),
        P(None, "dp", "mp"),
        P(None, "mp", "dp"),
        P("dp", None),
        P("dp", None),
        P("dp", None, None),
        P("dp", None, None),
        P(),
        P("dp", None, None),
        P("dp", None, None),
        P("dp", None, None),
        P("dp", None, None),
        P("dp", None, None),
        P("dp", None, None),
    )
    return jax.shard_map(
        on_device,
        mesh=mesh,
        in_specs=placed,
        out_specs=(
            P(("dp", "mp"), None, None),
            P("dp", "mp", None),
            P("dp", None, None),
            P("dp", None, None),
            P("dp", None, None),
            P("dp", None, None),
            P("dp", None, None),
        ),
        check_vma=False,
    )
```

profile of v0, /device:TPU:0, one launch (start us, length us, event | category | flops | bytes accessed | tf_op | source)
XLA Modules:
  0.0 542.9 jit_solution(12618972121489949078)
XLA Ops:
  11.4 1.9 fusion.54
  14.1 38.8 %all-gather = bf16[1,3,768,192]{3,1,0,2:T(4,128)(2,1)S(1)} all-gather(bf16[1,3,96,192]{3,1,0,2:T(4,128)(2,1)S(1)} %copy.243), channel_id=2, replica_groups=mesh['dp'=8,'mp'=4] {'dp'}, dimensions={2}, use_global_device_ids=true | all-gather | bytes 995328 | tf_op jit(solution)/shard_map/all_gather | solution.py:126
  52.9 2.0 copy.209
  54.9 5.2 all-gather.8
  61.5 32.1 %all-gather.1 = bf16[1,192,768]{1,0,2:T(2,128)(2,1)S(1)} all-gather(bf16[1,192,96]{1,0,2:T(2,128)(2,1)S(1)} %copy.244), channel_id=3, replica_groups=mesh['dp'=8,'mp'=4] {'dp'}, dimensions={2}, use_global_device_ids=true | all-gather | bytes 331776 | tf_op jit(solution)/shard_map/all_gather | solution.py:137
  95.6 2.2 fusion.118
  98.4 1.3 squeeze.46
  101.1 2.7 fusion.19
  103.8 2.1 fusion.20
  106.8 1.6 convolution_convert_fusion.3
  110.1 23.1 %reduce-scatter.5.cloned.1.call-done = bf16[192,768]{1,0:T(8,128)(2,1)} async-done(((bf16[768,768]{1,0:T(8,128)(2,1)}), bf16[192,768]{1,0:T(8,128)(2,1)}) %reduce-scatter.5.cloned.1.call-update) | async-done | bytes 294928 | tf_op jit(solution)/shard_map/reduce_scatter | solution.py:78
  136.5 15.6 %all-gather.26.cloned.1.call-done = bf16[1,768,768]{2,1,0:T(8,128)(2,1)} async-done(((bf16[1,96,768]{2,1,0:T(8,128)(2,1)}), bf16[1,768,768]{2,1,0:T(8,128)(2,1)}) %all-gather.26.cloned.1.call-update) | async-done | bytes 1179664 | tf_op jit(solution)/shard_map/all_gather | solution.py:145
  152.1 42.4 %all-gather.28.cloned.1.call-done = bf16[1,768,768]{1,2,0:T(8,128)(2,1)} async-done(((bf16[1,768,96]{1,2,0:T(8,128)(2,1)}), bf16[1,768,768]{1,2,0:T(8,128)(2,1)}) %all-gather.28.cloned.1.call-update) | async-done | bytes 1179664 | tf_op jit(solution)/shard_map/all_gather | solution.py:151
  194.5 17.7 %all-gather.20.cloned.1.call-done = bf16[768,768]{1,0:T(8,128)(2,1)} async-done(((bf16[192,768]{1,0:T(8,128)(2,1)}), bf16[768,768]{1,0:T(8,128)(2,1)}) %all-gather.20.cloned.1.call-update) | async-done | bytes 1179664 | tf_op jit(solution)/shard_map/all_gather | solution.py:72
  212.2 5.2 convolution_convert_fusion.2
  217.5 25.7 %reduce-scatter.7.cloned.1.call-done = bf16[192,768]{1,0:T(8,128)(2,1)} async-done(((bf16[768,768]{1,0:T(8,128)(2,1)}), bf16[192,768]{1,0:T(8,128)(2,1)}) %reduce-scatter.7.cloned.1.call-update) | async-done | bytes 294928 | tf_op jit(solution)/shard_map/reduce_scatter | solution.py:78
  245.7 38.6 %all-gather.4 = bf16[1,3,768,192]{3,1,0,2:T(4,128)(2,1)} all-gather(bf16[1,3,96,192]{3,1,0,2:T(4,128)(2,1)S(1)} %copy.245), channel_id=6, replica_groups=mesh['dp'=8,'mp'=4] {'dp'}, dimensions={2}, use_global_device_ids=true | all-gather | bytes 995328 | tf_op jit(solution)/shard_map/all_gather | solution.py:126
  284.3 3.4 copy.218
  287.8 32.2 %all-gather.5 = bf16[1,192,768]{1,0,2:T(2,128)(2,1)S(1)} all-gather(bf16[1,192,96]{1,0,2:T(2,128)(2,1)S(1)} %copy.246), channel_id=7, replica_groups=mesh['dp'=8,'mp'=4] {'dp'}, dimensions={2}, use_global_device_ids=true | all-gather | bytes 331776 | tf_op jit(solution)/shard_map/all_gather | solution.py:137
  320.6 2.4 fusion.119
  323.1 1.3 squeeze.52
  324.5 1.3 squeeze.53
  326.3 2.8 fusion.17
  329.1 2.9 fusion.21
  332.1 1.5 copy.223
  334.0 1.6 convolution_convert_fusion.1
  337.1 22.9 %reduce-scatter.9.cloned.1.call-done = bf16[192,768]{1,0:T(8,128)(2,1)} async-done(((bf16[768,768]{1,0:T(8,128)(2,1)}), bf16[192,768]{1,0:T(8,128)(2,1)}) %reduce-scatter.9.cloned.1.call-update) | async-done | bytes 294928 | tf_op jit(solution)/shard_map/reduce_scatter | solution.py:78
  363.3 15.3 %all-gather.30.cloned.1.call-done = bf16[1,768,768]{2,1,0:T(8,128)(2,1)} async-done(((bf16[1,96,768]{2,1,0:T(8,128)(2,1)}), bf16[1,768,768]{2,1,0:T(8,128)(2,1)}) %all-gather.30.cloned.1.call-update) | async-done | bytes 1179664 | tf_op jit(solution)/shard_map/all_gather | solution.py:145
  378.6 42.6 %all-gather.32.cloned.1.call-done = bf16[1,768,768]{1,2,0:T(8,128)(2,1)} async-done(((bf16[1,768,96]{1,2,0:T(8,128)(2,1)}), bf16[1,768,768]{1,2,0:T(8,128)(2,1)}) %all-gather.32.cloned.1.call-update) | async-done | bytes 1179664 | tf_op jit(solution)/shard_map/all_gather | solution.py:151
  421.2 17.7 %all-gather.24.cloned.1.call-done = bf16[768,768]{1,0:T(8,128)(2,1)} async-done(((bf16[192,768]{1,0:T(8,128)(2,1)}), bf16[768,768]{1,0:T(8,128)(2,1)}) %all-gather.24.cloned.1.call-update) | async-done | bytes 1179664 | tf_op jit(solution)/shard_map/all_gather | solution.py:72
  438.8 5.2 convolution_convert_fusion
  446.1 5.5 %all-to-all-start = ((s32[8,1,8]{2,1,0:T(1,128)}), s32[8,1,8]{2,1,0:T(1,128)S(1)}, u32[]{:S(2)}, u32[]{:S(2)}) async-start(s32[8,1,8]{2,1,0:T(1,128)} %bitcast.1), calls=%async_computation | async-start | bytes 8192 | tf_op jit(solution)/shard_map/all_to_all | solution.py:187
  453.0 2.1 scatter_fusion.1
  455.0 3.0 all-to-all-done
  458.0 3.3 all-to-all-start.3
  461.6 8.3 %reduce-scatter.11.cloned.1.call-done = bf16[192,768]{1,0:T(8,128)(2,1)} async-done(((bf16[768,768]{1,0:T(8,128)(2,1)}), bf16[192,768]{1,0:T(8,128)(2,1)}) %reduce-scatter.11.cloned.1.call-update) | async-done | bytes 294928 | tf_op jit(solution)/shard_map/reduce_scatter | solution.py:78
  472.4 2.2 fusion.117
  475.8 3.6 all-to-all-start.1
  479.6 3.4 all-to-all-done.1
  485.8 5.5 %all-to-all-start.2 = ((bf16[8,8,192]{2,1,0:T(8,128)(2,1)}), bf16[8,8,192]{2,1,0:T(8,128)(2,1)S(1)}, u32[]{:S(2)}, u32[]{:S(2)}) async-start(bf16[8,8,192]{2,1,0:T(8,128)(2,1)} %reshape.234), calls=%async_computation.6 | async-start | bytes 65536 | tf_op jit(solution)/shard_map/all_to_all | solution.py:173
  491.5 6.5 %all-to-all-done.2 = bf16[8,8,192]{2,1,0:T(8,128)(2,1)S(1)} async-done(((bf16[8,8,192]{2,1,0:T(8,128)(2,1)}), bf16[8,8,192]{2,1,0:T(8,128)(2,1)S(1)}, u32[]{:S(2)}, u32[]{:S(2)}) %all-to-all-start.2) | async-done | bytes 24608 | tf_op jit(solution)/shard_map/all_to_all | solution.py:173
  498.3 10.3 %psum.7 = bf16[4,16,256]{2,1,0:T(8,128)(2,1)S(1)} all-reduce(bf16[4,16,256]{2,1,0:T(8,128)(2,1)S(1)} %convolution_convert_fusion.10), channel_id=1, replica_groups=mesh['dp'=8,'mp'=4] {'mp'}, use_global_device_ids=true, to_apply=%region_19.20 | all-reduce | flops 16384 | bytes 65536 | tf_op jit(solution)/shard_map/psum | solution.py:222
  510.5 1.6 fusion.107
  512.6 1.6 fusion.105
  516.9 3.3 all-to-all-start.4
  521.1 5.7 %all-to-all-done.4 = bf16[8,8,192]{2,1,0:T(8,128)(2,1)S(1)} async-done(((bf16[8,8,192]{2,1,0:T(8,128)(2,1)}), bf16[8,8,192]{2,1,0:T(8,128)(2,1)S(1)}, u32[]{:S(2)}, u32[]{:S(2)}) %all-to-all-start.4) | async-done | bytes 24608 | tf_op jit(solution)/shard_map/all_to_all | solution.py:252
  528.0 3.2 all-to-all-start.5
  532.2 2.9 all-to-all-done.5
  (182 shorter events, 43.7 us)
Async XLA Ops:
  8.0 490.1 %copy-start = (bf16[4,768,256]{2,1,0:T(8,128)(2,1)S(1)}, bf16[4,768,256]{2,1,0:T(8,128)(2,1)}, u32[]{:S(2)}) copy-start(bf16[4,768,256]{2,1,0:T(8,128)(2,1)} %param.30) | copy-start | bytes 4718596
  8.0 5.3 copy-start.9
  8.0 87.6 %all-gather.18.cloned.1.call-start = ((), (), s32[]{:S(2)}) async-start(), calls=%async_computation.10 | async-start | bytes 1474560 | tf_op jit(solution)/shard_map/all_gather | solution.py:72
  13.3 119.9 %reduce-scatter.5.cloned.1.call-start = ((), (), s32[]{:S(2)}) async-start(), calls=%async_computation.11 | async-start | bytes 1474560 | tf_op jit(solution)/shard_map/reduce_scatter | solution.py:78
  52.9 2.0 copy-start.19
  52.9 7.8 %copy-start.14 = (bf16[2,192,96]{2,1,0:T(8,128)(2,1)S(1)}, bf16[2,192,96]{2,1,0:T(8,128)(2,1)}, u32[]{:S(2)}) copy-start(bf16[2,192,96]{2,1,0:T(8,128)(2,1)} %param.22) | copy-start | bytes 221188
  60.7 34.9 %copy-start.6 = (bf16[1,3,768,192]{2,3,1,0:T(8,128)(2,1)S(1)}, bf16[1,3,768,192]{2,3,1,0:T(8,128)(2,1)}, u32[]{:S(2)}) copy-start(bf16[1,3,768,192]{2,3,1,0:T(8,128)(2,1)} %copy.209) | copy-start | bytes 2654212
  98.4 2.7 copy-start.15
  101.1 2.7 copy-start.7
  106.7 1.6 copy-start.10
  108.3 1.0 copy-start.11
  108.3 24.9 %copy-start.1 = (bf16[192,768]{1,0:T(8,128)(2,1)S(1)}, bf16[192,768]{1,0:T(8,128)(2,1)}, u32[]{:S(2)}) copy-start(bf16[192,768]{1,0:T(8,128)(2,1)} %param.18) | copy-start | bytes 884740
  108.3 43.8 %all-gather.26.cloned.1.call-start = ((), (), s32[]{:S(2)}) async-start(), calls=%async_computation.18 | async-start | bytes 1327104 | tf_op jit(solution)/shard_map/all_gather | solution.py:145
  109.2 85.4 %all-gather.28.cloned.1.call-start = ((), (), s32[]{:S(2)}) async-start(), calls=%async_computation.19 | async-start | bytes 1327104 | tf_op jit(solution)/shard_map/all_gather | solution.py:151
  110.0 102.2 %all-gather.20.cloned.1.call-start = ((), (), s32[]{:S(2)}) async-start(), calls=%async_computation.12 | async-start | bytes 1474560 | tf_op jit(solution)/shard_map/all_gather | solution.py:72
  133.2 2.4 copy-start.2
  136.5 106.7 %reduce-scatter.7.cloned.1.call-start = ((), (), s32[]{:S(2)}) async-start(), calls=%async_computation.13 | async-start | bytes 1474560 | tf_op jit(solution)/shard_map/reduce_scatter | solution.py:78
  217.5 103.1 %all-gather.22.cloned.1.call-start = ((), (), s32[]{:S(2)}) async-start(), calls=%async_computation.14 | async-start | bytes 1474560 | tf_op jit(solution)/shard_map/all_gather | solution.py:72
  244.4 1.2 copy-start.8
  245.5 114.5 %reduce-scatter.9.cloned.1.call-start = ((), (), s32[]{:S(2)}) async-start(), calls=%async_computation.15 | async-start | bytes 1474560 | tf_op jit(solution)/shard_map/reduce_scatter | solution.py:78
  284.3 3.4 copy-start.12
  335.6 43.0 %all-gather.30.cloned.1.call-start = ((), (), s32[]{:S(2)}) async-start(), calls=%async_computation.20 | async-start | bytes 1327104 | tf_op jit(solution)/shard_map/all_gather | solution.py:145
  336.3 84.9 %all-gather.32.cloned.1.call-start = ((), (), s32[]{:S(2)}) async-start(), calls=%async_computation.21 | async-start | bytes 1327104 | tf_op jit(solution)/shard_map/all_gather | solution.py:151
  337.0 101.8 %all-gather.24.cloned.1.call-start = ((), (), s32[]{:S(2)}) async-start(), calls=%async_computation.16 | async-start | bytes 1474560 | tf_op jit(solution)/shard_map/all_gather | solution.py:72
  360.0 2.4 copy-start.3
  363.2 106.6 %reduce-scatter.11.cloned.1.call-start = ((), (), s32[]{:S(2)}) async-start(), calls=%async_computation.17 | async-start | bytes 1474560 | tf_op jit(solution)/shard_map/reduce_scatter | solution.py:78
  444.0 0.7 copy-start.20
  444.0 0.8 copy-start.22
  444.0 7.9 %copy-start.17 = (bf16[12,2,56]{2,1,0:T(2,128)(2,1)S(1)}, bf16[12,2,56]{2,1,0:T(2,128)(2,1)}, u32[]{:S(2)}) copy-start(bf16[12,2,56]{2,1,0:T(2,128)(2,1)} %param.28) | copy-start | bytes 8068
  444.0 7.9 %copy-start.18 = (bf16[12,2,56]{2,1,0:T(2,128)(2,1)S(1)}, bf16[12,2,56]{2,1,0:T(2,128)(2,1)}, u32[]{:S(2)}) copy-start(bf16[12,2,56]{2,1,0:T(2,128)(2,1)} %param.27) | copy-start | bytes 8068
  444.0 8.0 %copy-start.23 = (s32[25]{0:T(128)S(1)}, s32[25]{0:T(128)}, u32[]{:S(2)}) copy-start(s32[25]{0:T(128)} %param.29) | copy-start | bytes 304
  446.1 11.9 %all-to-all-start = ((s32[8,1,8]{2,1,0:T(1,128)}), s32[8,1,8]{2,1,0:T(1,128)S(1)}, u32[]{:S(2)}, u32[]{:S(2)}) async-start(s32[8,1,8]{2,1,0:T(1,128)} %bitcast.1), calls=%async_computation | async-start | bytes 8192 | tf_op jit(solution)/shard_map/all_to_all | solution.py:187
  458.0 17.7 %all-to-all-start.3 = ((bf16[8,8,112]{2,1,0:T(8,128)(2,1)}), bf16[8,8,112]{2,1,0:T(8,128)(2,1)S(1)}, u32[]{:S(2)}, u32[]{:S(2)}) async-start(bf16[8,8,112]{2,1,0:T(8,128)(2,1)} %bitcast.30), calls=%async_computation.7 | async-start | bytes 32768 | tf_op jit(solution)/shard_map/all_to_all | solution.py:180
  472.4 19.0 %copy-start.13 = (bf16[4,56,256]{2,1,0:T(8,128)(2,1)S(1)}, bf16[4,56,256]{2,1,0:T(8,128)(2,1)}, u32[]{:S(2)}) copy-start(bf16[4,56,256]{2,1,0:T(8,128)(2,1)} %param.31) | copy-start | bytes 344068
  474.6 34.0 %copy-start.16 = (bf16[4,20,256]{2,0,1:T(4,128)(2,1)S(1)}, bf16[4,20,256]{2,0,1:T(4,128)(2,1)}, u32[]{:S(2)}) copy-start(bf16[4,20,256]{2,0,1:T(4,128)(2,1)} %param.32) | copy-start | bytes 122884
  475.8 33.0 %copy-start.4 = (bf16[4,256,256]{2,1,0:T(8,128)(2,1)S(1)}, bf16[4,256,256]{2,1,0:T(8,128)(2,1)}, u32[]{:S(2)}) copy-start(bf16[4,256,256]{2,1,0:T(8,128)(2,1)} %param.33) | copy-start | bytes 1572868
  475.8 7.2 %all-to-all-start.1 = ((bf16[4,2,576]{2,1,0:T(2,128)(2,1)}), bf16[4,2,576]{2,1,0:T(2,128)(2,1)S(1)}, u32[]{:S(2)}, u32[]{:S(2)}) async-start(bf16[4,2,576]{2,1,0:T(2,128)(2,1)} %reshape.298), calls=%async_computation.5 | async-start | bytes 20480 | tf_op jit(solution)/shard_map/all_to_all | solution.py:163
  483.7 25.3 %copy-start.5 = (bf16[4,256,256]{2,1,0:T(8,128)(2,1)S(1)}, bf16[4,256,256]{2,1,0:T(8,128)(2,1)}, u32[]{:S(2)}) copy-start(bf16[4,256,256]{2,1,0:T(8,128)(2,1)} %param.34) | copy-start | bytes 1572868
  485.8 12.2 %all-to-all-start.2 = ((bf16[8,8,192]{2,1,0:T(8,128)(2,1)}), bf16[8,8,192]{2,1,0:T(8,128)(2,1)S(1)}, u32[]{:S(2)}, u32[]{:S(2)}) async-start(bf16[8,8,192]{2,1,0:T(8,128)(2,1)} %reshape.234), calls=%async_computation.6 | async-start | bytes 65536 | tf_op jit(solution)/shard_map/all_to_all | solution.py:173
  491.5 17.7 %copy-start.21 = (bf16[4,256,56]{1,2,0:T(8,128)(2,1)S(1)}, bf16[4,256,56]{1,2,0:T(8,128)(2,1)}, u32[]{:S(2)}) copy-start(bf16[4,256,56]{1,2,0:T(8,128)(2,1)} %param.35) | copy-start | bytes 344068
  516.9 10.0 %all-to-all-start.4 = ((bf16[8,8,192]{2,1,0:T(8,128)(2,1)}), bf16[8,8,192]{2,1,0:T(8,128)(2,1)S(1)}, u32[]{:S(2)}, u32[]{:S(2)}) async-start(bf16[8,8,192]{2,1,0:T(8,128)(2,1)} %copy.237), calls=%async_computation.8 | async-start | bytes 65536 | tf_op jit(solution)/shard_map/all_to_all | solution.py:252
  528.0 7.1 %all-to-all-start.5 = ((bf16[12,2,192]{2,1,0:T(2,128)(2,1)}), bf16[12,2,192]{2,1,0:T(2,128)(2,1)S(1)}, u32[]{:S(2)}, u32[]{:S(2)}) async-start(bf16[12,2,192]{2,1,0:T(2,128)(2,1)} %gather_fusion), calls=%async_computation.9 | async-start | bytes 24576 | tf_op jit(solution)/shard_map/all_to_all | solution.py:254
Sparse Core Ops, SparseCore 0:
  13.4 20.1 all-gather.17
  108.5 24.7 reduce-scatter.4
  217.6 25.6 reduce-scatter.6
  335.7 24.2 reduce-scatter.8
  444.2 25.6 reduce-scatter.10
Sparse Core Ops, SparseCore 1:
  111.6 40.5 all-gather.25
  154.8 39.7 all-gather.27
  196.5 15.6 all-gather.19
  245.6 17.3 all-gather.21
  338.5 40.0 all-gather.29
  381.4 39.7 all-gather.31
  423.2 15.6 all-gather.23
where the time goes:
time: 544 us; the launch traced here: 543 us
  waiting for transfers between devices  254 us (47%)
  blocking collectives  157 us (29%)
  matrix products  37.6 us (7%)
  local copies, waits for them, and re-layouts  33.4 us (6%)
  starting transfers between devices  25.1 us (5%)
  other arithmetic  19.4 us (4%)
  between operations  15.9 us (3%)
    all_gather x2, waiting for transfers between devices, on_device(): lax.all_gather(mlp_out[layer_index], 'dp', axis=1, tiled=True)  85 us
    reduce_scatter x4, waiting for transfers between devices, reduce_rows(): lax.psum_scatter(partial_value.astype(jnp.bfloat16), 'mp', scatter_dimens...  80 us
    all_gather x2, blocking collectives, on_device(): lax.all_gather(attn_in[layer_index], 'dp', axis=1, tiled=True)  77.4 us
    all_gather x2, blocking collectives, on_device(): lax.all_gather(attn_out[layer_index], 'dp', axis=1, tiled=True)  64.3 us
    all_gather x4, waiting for transfers between devices, gather_rows(): lax.all_gather(normed, 'mp', axis=0, tiled=True)  35.4 us
    all_gather x2, waiting for transfers between devices, on_device(): lax.all_gather(mlp_in[layer_index], 'dp', axis=0, tiled=True)  30.9 us
  transfers between devices with their start and end apart: 18, of which 15 were waited for; matrix products, arithmetic and copies ran while one was open for 6% of the time, Pallas kernels for 0%

commit v1 on v0

--- a/solution.py
+++ b/solution.py
@@ -12,6 +12,22 @@
 ADIM_MAX = 14
 ACT = 56
 norm_eps = 1e-05
+
+
+def ring_product(value, axis, dim, term):
+    size, index, rows = (lax.axis_size(axis), lax.axis_index(axis), value.shape[dim])
+    forward = [(i, (i + 1) % size) for i in range(size)]
+    left = [(i, (i - 1) % size) for i in range(size)]
+    halfway = size // 2
+    from_left = from_right = value
+    total = term(value, index * rows)
+    for step in range(1, halfway + 1):
+        from_left = lax.ppermute(from_left, axis, forward)
+        if step < size - halfway:
+            from_right = lax.ppermute(from_right, axis, left)
+            total = total + term(from_right, (index + step) % size * rows)
+        total = total + term(from_left, (index - step) % size * rows)
+    return total
 
 
 def normalize(values, scale_gain):
@@ -120,11 +136,16 @@
         gathered, mask_group = gather_rows(normed, obs_mask)
         samples_group = mask_group.shape[0]
         columns = gathered
-        projected = jnp.einsum(
-            "td,jdc->jtc",
-            columns,
-            lax.all_gather(attn_in[layer_index], "dp", axis=1, tiled=True),
-            preferred_element_type=jnp.float32,
+        projected = ring_product(
+            attn_in[layer_index],
+            "dp",
+            1,
+            lambda part, start: jnp.einsum(
+                "td,jdc->jtc",
+                lax.dynamic_slice_in_dim(columns, start, part.shape[1], axis=1),
+                part,
+                preferred_element_type=jnp.float32,
+            ),
         )
         projected = projected.astype(jnp.bfloat16).reshape(
             3, samples_group, length, heads_local, HDIM

time: 544 us -> 523 us (0.961)
  blocking collectives: 157 us -> 81.9 us
  starting transfers between devices: 25.1 us -> 56.1 us
  waiting for transfers between devices: 254 us -> 276 us
  matrix products: 37.6 us -> 45.8 us
  local copies, waits for them, and re-layouts: 33.4 us -> 27.7 us
    all_gather x2 -> x0, blocking collectives: 77.4 us -> none  [on_device(): lax.all_gather(attn_in[layer_index], 'dp', axis=1, tiled=True)]
    ppermute x0 -> x14, starting transfers between devices: none -> 30.8 us  [the longest x6 26.6 us: ring_product(): from_right = lax.ppermute(from_right, axis, left)]
    ppermute x0 -> x14, waiting for transfers between devices: none -> 17.6 us  [the longest x8 11.2 us: ring_product(): from_left = lax.ppermute(from_left, axis, forward)]
    unnamed x2 -> x16, matrix products: 4.58 us -> 12.6 us
  transfers between devices with their start and end apart: 18 -> 32, of which waited for: 15 -> 21; matrix products, arithmetic and copies ran while one was open for 6% -> 6% of each run, Pallas kernels for 0% -> 0%
where the time goes in v1:
time: 523 us; the launch traced here: 521 us
  waiting for transfers between devices  276 us (53%)
  blocking collectives  81.9 us (16%)
  starting transfers between devices  56.1 us (11%)
  matrix products  45.8 us (9%)
  local copies, waits for them, and re-layouts  27.7 us (5%)
  other arithmetic  17.7 us (3%)
  between operations  16.1 us (3%)
    all_gather x2, waiting for transfers between devices, on_device(): lax.all_gather(mlp_out[layer_index], 'dp', axis=1, tiled=True)  85 us
    reduce_scatter x4, waiting for transfers between devices, reduce_rows(): lax.psum_scatter(partial_value.astype(jnp.bfloat16), 'mp', scatter_dimens...  84.4 us
    all_gather x2, blocking collectives, on_device(): lax.all_gather(attn_out[layer_index], 'dp', axis=1, tiled=True)  66.5 us
    all_gather x4, waiting for transfers between devices, gather_rows(): lax.all_gather(normed, 'mp', axis=0, tiled=True)  35.4 us
    all_gather x2, waiting for transfers between devices, on_device(): lax.all_gather(mlp_in[layer_index], 'dp', axis=0, tiled=True)  30.5 us
    ppermute x6, starting transfers between devices, ring_product(): from_right = lax.ppermute(from_right, axis, left)  26.6 us
    unnamed x16, matrix products  12.6 us
    ppermute x8, waiting for transfers between devices, ring_product(): from_left = lax.ppermute(from_left, axis, forward)  11.2 us
  transfers between devices with their start and end apart: 32, of which 21 were waited for; matrix products, arithmetic and copies ran while one was open for 6% of the time, Pallas kernels for 0%

profile of v1, /device:TPU:0, one launch (start us, length us, event | category | flops | bytes accessed | tf_op | source)
XLA Modules:
  0.0 521.5 jit_solution(13579531374184712711)
XLA Ops:
  11.4 1.9 fusion.56
  14.2 3.0 collective-permute-start.1
  17.3 3.1 collective-permute-start
  20.4 5.2 all-gather.6
  26.3 8.8 %collective-permute-done.3 = bf16[3,96,192]{1,2,0:T(8,128)(2,1)S(1)} collective-permute-done((bf16[3,96,192]{1,2,0:T(8,128)(2,1)S(1)}, bf16[3,96,192]{1,2,0:T(8,128)(2,1)S(1)}, u32[]{:S(2)}, u32[]{:S(2)}) %collective-permute-start.3) | collective-permute-done | bytes 110624 | tf_op jit(solution)/shard_map/ppermute | solution.py:25
  36.0 4.8 collective-permute-start.2
  40.8 2.3 collective-permute-done.5
  43.8 32.7 %all-gather = bf16[1,192,768]{1,0,2:T(2,128)(2,1)S(1)} all-gather(bf16[1,192,96]{1,0,2:T(2,128)(2,1)S(1)} %copy.361), channel_id=2, replica_groups=mesh['dp'=8,'mp'=4] {'dp'}, dimensions={2}, use_global_device_ids=true | all-gather | bytes 331776 | tf_op jit(solution)/shard_map/all_gather | solution.py:158
  77.0 3.8 collective-permute-start.4
  80.8 1.6 fusion.88
  91.0 2.6 fusion.19
  93.7 2.3 fusion.20
  100.1 26.0 %reduce-scatter.13.cloned.1.call-done = bf16[192,768]{1,0:T(8,128)(2,1)} async-done(((bf16[768,768]{1,0:T(8,128)(2,1)}), bf16[192,768]{1,0:T(8,128)(2,1)}) %reduce-scatter.13.cloned.1.call-update) | async-done | bytes 294928 | tf_op jit(solution)/shard_map/reduce_scatter | solution.py:94
  129.7 15.4 %all-gather.24.cloned.1.call-done = bf16[1,768,768]{2,1,0:T(8,128)(2,1)} async-done(((bf16[1,96,768]{2,1,0:T(8,128)(2,1)}), bf16[1,768,768]{2,1,0:T(8,128)(2,1)}) %all-gather.24.cloned.1.call-update) | async-done | bytes 1179664 | tf_op jit(solution)/shard_map/all_gather | solution.py:166
  145.1 42.4 %all-gather.26.cloned.1.call-done = bf16[1,768,768]{1,2,0:T(8,128)(2,1)} async-done(((bf16[1,768,96]{1,2,0:T(8,128)(2,1)}), bf16[1,768,768]{1,2,0:T(8,128)(2,1)}) %all-gather.26.cloned.1.call-update) | async-done | bytes 1179664 | tf_op jit(solution)/shard_map/all_gather | solution.py:172
  187.5 17.7 %all-gather.18.cloned.1.call-done = bf16[768,768]{1,0:T(8,128)(2,1)} async-done(((bf16[192,768]{1,0:T(8,128)(2,1)}), bf16[768,768]{1,0:T(8,128)(2,1)}) %all-gather.18.cloned.1.call-update) | async-done | bytes 1179664 | tf_op jit(solution)/shard_map/all_gather | solution.py:88
  205.2 5.2 convolution_convert_fusion.2
  210.5 25.7 %reduce-scatter.15.cloned.1.call-done = bf16[192,768]{1,0:T(8,128)(2,1)} async-done(((bf16[768,768]{1,0:T(8,128)(2,1)}), bf16[192,768]{1,0:T(8,128)(2,1)}) %reduce-scatter.15.cloned.1.call-update) | async-done | bytes 294928 | tf_op jit(solution)/shard_map/reduce_scatter | solution.py:94
  238.8 4.3 collective-permute-start.7
  243.0 2.9 collective-permute-done.7
  246.0 5.3 %collective-permute-start.9 = (bf16[3,96,192]{1,2,0:T(8,128)(2,1)S(1)}, bf16[3,96,192]{1,2,0:T(8,128)(2,1)}, u32[]{:S(2)}, u32[]{:S(2)}) collective-permute-start(bf16[3,96,192]{1,2,0:T(8,128)(2,1)S(1)} %collective-permute-done.7), channel_id=1, source_target_pairs={{0,28},{4,0},{8,4},{12,8},{16,12},{20,16},{24,20},{28,24},{1,29},{... | collective-permute-start | bytes 331784 | tf_op jit(solution)/shard_map/ppermute | solution.py:27
  251.5 2.5 collective-permute-done.9
  253.9 5.4 %collective-permute-start.11 = (bf16[3,96,192]{1,2,0:T(8,128)(2,1)}, bf16[3,96,192]{1,2,0:T(8,128)(2,1)}, u32[]{:S(2)}, u32[]{:S(2)}) collective-permute-start(bf16[3,96,192]{1,2,0:T(8,128)(2,1)} %collective-permute-done.9), channel_id=1, source_target_pairs={{0,28},{4,0},{8,4},{12,8},{16,12},{20,16},{24,20},{28,24},{1,29},{... | collective-permute-start | bytes 331784 | tf_op jit(solution)/shard_map/ppermute | solution.py:27
  259.3 33.8 %all-gather.3 = bf16[1,192,768]{1,0,2:T(2,128)(2,1)S(1)} all-gather(bf16[1,192,96]{1,0,2:T(2,128)(2,1)S(1)} %copy.371), channel_id=5, replica_groups=mesh['dp'=8,'mp'=4] {'dp'}, dimensions={2}, use_global_device_ids=true | all-gather | bytes 331776 | tf_op jit(solution)/shard_map/all_gather | solution.py:158
  294.0 1.6 fusion.76
  306.4 2.9 fusion.17
  309.3 2.9 fusion.21
  317.2 24.4 %reduce-scatter.17.cloned.1.call-done = bf16[192,768]{1,0:T(8,128)(2,1)} async-done(((bf16[768,768]{1,0:T(8,128)(2,1)}), bf16[192,768]{1,0:T(8,128)(2,1)}) %reduce-scatter.17.cloned.1.call-update) | async-done | bytes 294928 | tf_op jit(solution)/shard_map/reduce_scatter | solution.py:94
  345.1 15.1 %all-gather.28.cloned.1.call-done = bf16[1,768,768]{2,1,0:T(8,128)(2,1)} async-done(((bf16[1,96,768]{2,1,0:T(8,128)(2,1)}), bf16[1,768,768]{2,1,0:T(8,128)(2,1)}) %all-gather.28.cloned.1.call-update) | async-done | bytes 1179664 | tf_op jit(solution)/shard_map/all_gather | solution.py:166
  360.1 42.6 %all-gather.30.cloned.1.call-done = bf16[1,768,768]{1,2,0:T(8,128)(2,1)} async-done(((bf16[1,768,96]{1,2,0:T(8,128)(2,1)}), bf16[1,768,768]{1,2,0:T(8,128)(2,1)}) %all-gather.30.cloned.1.call-update) | async-done | bytes 1179664 | tf_op jit(solution)/shard_map/all_gather | solution.py:172
  402.7 17.7 %all-gather.22.cloned.1.call-done = bf16[768,768]{1,0:T(8,128)(2,1)} async-done(((bf16[192,768]{1,0:T(8,128)(2,1)}), bf16[768,768]{1,0:T(8,128)(2,1)}) %all-gather.22.cloned.1.call-update) | async-done | bytes 1179664 | tf_op jit(solution)/shard_map/all_gather | solution.py:88
  420.4 5.2 convolution_convert_fusion
  427.7 5.5 %all-to-all-start = ((s32[8,1,8]{2,1,0:T(1,128)}), s32[8,1,8]{2,1,0:T(1,128)S(1)}, u32[]{:S(2)}, u32[]{:S(2)}) async-start(s32[8,1,8]{2,1,0:T(1,128)} %bitcast.1), calls=%async_computation | async-start | bytes 8192 | tf_op jit(solution)/shard_map/all_to_all | solution.py:208
  434.5 2.1 scatter_fusion.1
  436.6 3.0 all-to-all-done
  439.6 3.3 all-to-all-start.3
  443.1 8.3 %reduce-scatter.19.cloned.1.call-done = bf16[192,768]{1,0:T(8,128)(2,1)} async-done(((bf16[768,768]{1,0:T(8,128)(2,1)}), bf16[192,768]{1,0:T(8,128)(2,1)}) %reduce-scatter.19.cloned.1.call-update) | async-done | bytes 294928 | tf_op jit(solution)/shard_map/reduce_scatter | solution.py:94
  454.4 3.4 all-to-all-start.1
  458.0 3.6 all-to-all-done.1
  464.3 5.5 %all-to-all-start.2 = ((bf16[8,8,192]{2,1,0:T(8,128)(2,1)}), bf16[8,8,192]{2,1,0:T(8,128)(2,1)S(1)}, u32[]{:S(2)}, u32[]{:S(2)}) async-start(bf16[8,8,192]{2,1,0:T(8,128)(2,1)} %reshape.234), calls=%async_computation.2 | async-start | bytes 65536 | tf_op jit(solution)/shard_map/all_to_all | solution.py:194
  470.0 6.5 %all-to-all-done.2 = bf16[8,8,192]{2,1,0:T(8,128)(2,1)S(1)} async-done(((bf16[8,8,192]{2,1,0:T(8,128)(2,1)}), bf16[8,8,192]{2,1,0:T(8,128)(2,1)S(1)}, u32[]{:S(2)}, u32[]{:S(2)}) %all-to-all-start.2) | async-done | bytes 24608 | tf_op jit(solution)/shard_map/all_to_all | solution.py:194
  476.8 10.3 %psum.7 = bf16[4,16,256]{2,1,0:T(8,128)(2,1)S(1)} all-reduce(bf16[4,16,256]{2,1,0:T(8,128)(2,1)S(1)} %convolution_convert_fusion.10), channel_id=1, replica_groups=mesh['dp'=8,'mp'=4] {'mp'}, use_global_device_ids=true, to_apply=%region_19.20 | all-reduce | flops 16384 | bytes 65536 | tf_op jit(solution)/shard_map/psum | solution.py:243
  489.1 1.6 fusion.157
  491.2 1.6 fusion.155
  495.4 3.3 all-to-all-start.4
  499.7 5.7 %all-to-all-done.4 = bf16[8,8,192]{2,1,0:T(8,128)(2,1)S(1)} async-done(((bf16[8,8,192]{2,1,0:T(8,128)(2,1)}), bf16[8,8,192]{2,1,0:T(8,128)(2,1)S(1)}, u32[]{:S(2)}, u32[]{:S(2)}) %all-to-all-start.4) | async-done | bytes 24608 | tf_op jit(solution)/shard_map/all_to_all | solution.py:273
  506.6 3.2 all-to-all-start.5
  510.8 2.9 all-to-all-done.5
  (222 shorter events, 64.4 us)
Async XLA Ops:
  8.0 468.7 %copy-start = (bf16[4,768,256]{2,1,0:T(8,128)(2,1)S(1)}, bf16[4,768,256]{2,1,0:T(8,128)(2,1)}, u32[]{:S(2)}) copy-start(bf16[4,768,256]{2,1,0:T(8,128)(2,1)} %param.30) | copy-start | bytes 4718596
  8.0 5.4 %copy-start.9 = (bf16[2,3,96,192]{3,2,1,0:T(8,128)(2,1)S(1)}, bf16[2,3,96,192]{3,2,1,0:T(8,128)(2,1)}, u32[]{:S(2)}) copy-start(bf16[2,3,96,192]{3,2,1,0:T(8,128)(2,1)} %param.21) | copy-start | bytes 663556
  8.0 72.8 %all-gather.16.cloned.1.call-start = ((), (), s32[]{:S(2)}) async-start(), calls=%async_computation.10 | async-start | bytes 1474560 | tf_op jit(solution)/shard_map/all_gather | solution.py:88
  9.1 11.3 %copy-start.21 = (s32[3,64]{1,0:T(4,128)S(1)}, s32[3,64]{1,0:T(4,128)}, u32[]{:S(2)}) copy-start(s32[3,64]{1,0:T(4,128)} %param.19) | copy-start | bytes 2308
  9.1 16.5 %copy-start.16 = (bf16[2,192,96]{2,1,0:T(8,128)(2,1)S(1)}, bf16[2,192,96]{2,1,0:T(8,128)(2,1)}, u32[]{:S(2)}) copy-start(bf16[2,192,96]{2,1,0:T(8,128)(2,1)} %param.22) | copy-start | bytes 221188
  13.3 112.9 %reduce-scatter.13.cloned.1.call-start = ((), (), s32[]{:S(2)}) async-start(), calls=%async_computation.18 | async-start | bytes 1474560 | tf_op jit(solution)/shard_map/reduce_scatter | solution.py:94
  14.2 12.0 %collective-permute-start.1 = (bf16[3,96,192]{1,2,0:T(8,128)(2,1)S(1)}, bf16[3,96,192]{1,2,0:T(8,128)(2,1)S(1)}, u32[]{:S(2)}, u32[]{:S(2)}) collective-permute-start(bf16[3,96,192]{1,2,0:T(8,128)(2,1)S(1)} %bitcast.213), channel_id=1, source_target_pairs={{0,4},{4,8},{8,12},{12,16},{16,20},{20,24},{24,28},{28,0},{1,5},{5... | collective-permute-start | bytes 331784 | tf_op jit(solution)/shard_map/ppermute | solution.py:25
  17.3 18.7 %collective-permute-start = (bf16[3,96,192]{1,2,0:T(8,128)(2,1)S(1)}, bf16[3,96,192]{1,2,0:T(8,128)(2,1)S(1)}, u32[]{:S(2)}, u32[]{:S(2)}) collective-permute-start(bf16[3,96,192]{1,2,0:T(8,128)(2,1)S(1)} %bitcast.214), channel_id=1, source_target_pairs={{0,28},{4,0},{8,4},{12,8},{16,12},{20,16},{24,20},{28,24},{1,29},{... | collective-permute-start | bytes 331784 | tf_op jit(solution)/shard_map/ppermute | solution.py:27
  26.2 8.8 %collective-permute-start.3 = (bf16[3,96,192]{1,2,0:T(8,128)(2,1)S(1)}, bf16[3,96,192]{1,2,0:T(8,128)(2,1)S(1)}, u32[]{:S(2)}, u32[]{:S(2)}) collective-permute-start(bf16[3,96,192]{1,2,0:T(8,128)(2,1)S(1)} %collective-permute-done.1), channel_id=1, source_target_pairs={{0,4},{4,8},{8,12},{12,16},{16,20},{20,24},{24,28},{28,0},{1,5},{5... | collective-permute-start | bytes 331784 | tf_op jit(solution)/shard_map/ppermute | solution.py:25
  35.1 8.0 %collective-permute-start.5 = (bf16[3,96,192]{1,2,0:T(8,128)(2,1)S(1)}, bf16[3,96,192]{1,2,0:T(8,128)(2,1)S(1)}, u32[]{:S(2)}, u32[]{:S(2)}) collective-permute-start(bf16[3,96,192]{1,2,0:T(8,128)(2,1)S(1)} %collective-permute-done.3), channel_id=1, source_target_pairs={{0,4},{4,8},{8,12},{12,16},{16,20},{20,24},{24,28},{28,0},{1,5},{5... | collective-permute-start | bytes 331784 | tf_op jit(solution)/shard_map/ppermute | solution.py:25
  36.0 40.9 %collective-permute-start.2 = (bf16[3,96,192]{1,2,0:T(8,128)(2,1)S(1)}, bf16[3,96,192]{1,2,0:T(8,128)(2,1)S(1)}, u32[]{:S(2)}, u32[]{:S(2)}) collective-permute-start(bf16[3,96,192]{1,2,0:T(8,128)(2,1)S(1)} %collective-permute-done), channel_id=1, source_target_pairs={{0,28},{4,0},{8,4},{12,8},{16,12},{20,16},{24,20},{28,24},{1,29},{... | collective-permute-start | bytes 331784 | tf_op jit(solution)/shard_map/ppermute | solution.py:27
  43.1 37.7 %collective-permute-start.6 = (bf16[3,96,192]{1,2,0:T(8,128)(2,1)S(1)}, bf16[3,96,192]{1,2,0:T(8,128)(2,1)}, u32[]{:S(2)}, u32[]{:S(2)}) collective-permute-start(bf16[3,96,192]{1,2,0:T(8,128)(2,1)S(1)} %collective-permute-done.5), channel_id=1, source_target_pairs={{0,4},{4,8},{8,12},{12,16},{16,20},{20,24},{24,28},{28,0},{1,5},{5... | collective-permute-start | bytes 331784 | tf_op jit(solution)/shard_map/ppermute | solution.py:25
  77.0 6.5 %collective-permute-start.4 = (bf16[3,96,192]{1,2,0:T(8,128)(2,1)S(1)}, bf16[3,96,192]{1,2,0:T(8,128)(2,1)S(1)}, u32[]{:S(2)}, u32[]{:S(2)}) collective-permute-start(bf16[3,96,192]{1,2,0:T(8,128)(2,1)S(1)} %collective-permute-done.2), channel_id=1, source_target_pairs={{0,28},{4,0},{8,4},{12,8},{16,12},{20,16},{24,20},{28,24},{1,29},{... | collective-permute-start | bytes 331784 | tf_op jit(solution)/shard_map/ppermute | solution.py:27
  88.3 2.7 copy-start.17
  98.4 27.8 %copy-start.1 = (bf16[192,768]{1,0:T(8,128)(2,1)S(1)}, bf16[192,768]{1,0:T(8,128)(2,1)}, u32[]{:S(2)}) copy-start(bf16[192,768]{1,0:T(8,128)(2,1)} %param.18) | copy-start | bytes 884740
  98.4 46.7 %all-gather.24.cloned.1.call-start = ((), (), s32[]{:S(2)}) async-start(), calls=%async_computation.14 | async-start | bytes 1327104 | tf_op jit(solution)/shard_map/all_gather | solution.py:166
  99.2 88.3 %all-gather.26.cloned.1.call-start = ((), (), s32[]{:S(2)}) async-start(), calls=%async_computation.15 | async-start | bytes 1327104 | tf_op jit(solution)/shard_map/all_gather | solution.py:172
  100.1 105.1 %all-gather.18.cloned.1.call-start = ((), (), s32[]{:S(2)}) async-start(), calls=%async_computation.11 | async-start | bytes 1474560 | tf_op jit(solution)/shard_map/all_gather | solution.py:88
  129.5 106.8 %reduce-scatter.15.cloned.1.call-start = ((), (), s32[]{:S(2)}) async-start(), calls=%async_computation.19 | async-start | bytes 1474560 | tf_op jit(solution)/shard_map/reduce_scatter | solution.py:94
  210.5 83.5 %all-gather.20.cloned.1.call-start = ((), (), s32[]{:S(2)}) async-start(), calls=%async_computation.12 | async-start | bytes 1474560 | tf_op jit(solution)/shard_map/all_gather | solution.py:88
  237.4 14.0 %copy-start.12 = (bf16[1,192,96]{2,1,0:T(8,128)(2,1)S(1)}, bf16[1,192,96]{2,1,0:T(8,128)(2,1)}, u32[]{:S(2)}) copy-start(bf16[1,192,96]{2,1,0:T(8,128)(2,1)} %get-tuple-element.75) | copy-start | bytes 110596
  238.5 103.0 %reduce-scatter.17.cloned.1.call-start = ((), (), s32[]{:S(2)}) async-start(), calls=%async_computation.20 | async-start | bytes 1474560 | tf_op jit(solution)/shard_map/reduce_scatter | solution.py:94
  238.8 7.2 %collective-permute-start.7 = (bf16[3,96,192]{1,2,0:T(8,128)(2,1)S(1)}, bf16[3,96,192]{1,2,0:T(8,128)(2,1)S(1)}, u32[]{:S(2)}, u32[]{:S(2)}) collective-permute-start(bf16[3,96,192]{1,2,0:T(8,128)(2,1)S(1)} %bitcast.216), channel_id=1, source_target_pairs={{0,28},{4,0},{8,4},{12,8},{16,12},{20,16},{24,20},{28,24},{1,29},{... | collective-permute-start | bytes 331784 | tf_op jit(solution)/shard_map/ppermute | solution.py:27
  243.0 8.2 %collective-permute-start.8 = (bf16[3,96,192]{1,2,0:T(8,128)(2,1)S(1)}, bf16[3,96,192]{1,2,0:T(8,128)(2,1)S(1)}, u32[]{:S(2)}, u32[]{:S(2)}) collective-permute-start(bf16[3,96,192]{1,2,0:T(8,128)(2,1)S(1)} %bitcast.217), channel_id=1, source_target_pairs={{0,4},{4,8},{8,12},{12,16},{16,20},{20,24},{24,28},{28,0},{1,5},{5... | collective-permute-start | bytes 331784 | tf_op jit(solution)/shard_map/ppermute | solution.py:25
  246.0 8.0 %collective-permute-start.9 = (bf16[3,96,192]{1,2,0:T(8,128)(2,1)S(1)}, bf16[3,96,192]{1,2,0:T(8,128)(2,1)}, u32[]{:S(2)}, u32[]{:S(2)}) collective-permute-start(bf16[3,96,192]{1,2,0:T(8,128)(2,1)S(1)} %collective-permute-done.7), channel_id=1, source_target_pairs={{0,28},{4,0},{8,4},{12,8},{16,12},{20,16},{24,20},{28,24},{1,29},{... | collective-permute-start | bytes 331784 | tf_op jit(solution)/shard_map/ppermute | solution.py:27
  251.3 8.1 %copy-start.13 = (bf16[3,96,192]{1,2,0:T(8,128)(2,1)}, bf16[3,96,192]{1,2,0:T(8,128)(2,1)S(1)}, u32[]{:S(2)}) copy-start(bf16[3,96,192]{1,2,0:T(8,128)(2,1)S(1)} %collective-permute-done.8) | copy-start | bytes 331780
  251.3 8.0 %collective-permute-start.10 = (bf16[3,96,192]{1,2,0:T(8,128)(2,1)S(1)}, bf16[3,96,192]{1,2,0:T(8,128)(2,1)}, u32[]{:S(2)}, u32[]{:S(2)}) collective-permute-start(bf16[3,96,192]{1,2,0:T(8,128)(2,1)S(1)} %collective-permute-done.8), channel_id=1, source_target_pairs={{0,4},{4,8},{8,12},{12,16},{16,20},{20,24},{24,28},{28,0},{1,5},{5... | collective-permute-start | bytes 331784 | tf_op jit(solution)/shard_map/ppermute | solution.py:25
  253.9 40.0 %collective-permute-start.11 = (bf16[3,96,192]{1,2,0:T(8,128)(2,1)}, bf16[3,96,192]{1,2,0:T(8,128)(2,1)}, u32[]{:S(2)}, u32[]{:S(2)}) collective-permute-start(bf16[3,96,192]{1,2,0:T(8,128)(2,1)} %collective-permute-done.9), channel_id=1, source_target_pairs={{0,28},{4,0},{8,4},{12,8},{16,12},{20,16},{24,20},{28,24},{1,29},{... | collective-permute-start | bytes 331784 | tf_op jit(solution)/shard_map/ppermute | solution.py:27
  259.3 34.3 %collective-permute-start.12 = (bf16[3,96,192]{1,2,0:T(8,128)(2,1)}, bf16[3,96,192]{1,2,0:T(8,128)(2,1)}, u32[]{:S(2)}, u32[]{:S(2)}) collective-permute-start(bf16[3,96,192]{1,2,0:T(8,128)(2,1)} %collective-permute-done.10), channel_id=1, source_target_pairs={{0,4},{4,8},{8,12},{12,16},{16,20},{20,24},{24,28},{28,0},{1,5},{5... | collective-permute-start | bytes 331784 | tf_op jit(solution)/shard_map/ppermute | solution.py:25
  293.6 8.1 %collective-permute-start.13 = (bf16[3,96,192]{1,2,0:T(8,128)(2,1)}, bf16[3,96,192]{1,2,0:T(8,128)(2,1)S(1)}, u32[]{:S(2)}, u32[]{:S(2)}) collective-permute-start(bf16[3,96,192]{1,2,0:T(8,128)(2,1)} %collective-permute-done.12), channel_id=1, source_target_pairs={{0,4},{4,8},{8,12},{12,16},{16,20},{20,24},{24,28},{28,0},{1,5},{5... | collective-permute-start | bytes 331784 | tf_op jit(solution)/shard_map/ppermute | solution.py:25
  315.6 44.5 %all-gather.28.cloned.1.call-start = ((), (), s32[]{:S(2)}) async-start(), calls=%async_computation.16 | async-start | bytes 1327104 | tf_op jit(solution)/shard_map/all_gather | solution.py:166
  316.4 86.3 %all-gather.30.cloned.1.call-start = ((), (), s32[]{:S(2)}) async-start(), calls=%async_computation.17 | async-start | bytes 1327104 | tf_op jit(solution)/shard_map/all_gather | solution.py:172
  317.1 103.3 %all-gather.22.cloned.1.call-start = ((), (), s32[]{:S(2)}) async-start(), calls=%async_computation.13 | async-start | bytes 1474560 | tf_op jit(solution)/shard_map/all_gather | solution.py:88
  344.8 106.6 %reduce-scatter.19.cloned.1.call-start = ((), (), s32[]{:S(2)}) async-start(), calls=%async_computation.21 | async-start | bytes 1474560 | tf_op jit(solution)/shard_map/reduce_scatter | solution.py:94
  425.6 7.9 %copy-start.19 = (bf16[12,2,56]{2,1,0:T(2,128)(2,1)S(1)}, bf16[12,2,56]{2,1,0:T(2,128)(2,1)}, u32[]{:S(2)}) copy-start(bf16[12,2,56]{2,1,0:T(2,128)(2,1)} %param.28) | copy-start | bytes 8068
  425.6 7.9 %copy-start.20 = (bf16[12,2,56]{2,1,0:T(2,128)(2,1)S(1)}, bf16[12,2,56]{2,1,0:T(2,128)(2,1)}, u32[]{:S(2)}) copy-start(bf16[12,2,56]{2,1,0:T(2,128)(2,1)} %param.27) | copy-start | bytes 8068
  425.6 8.1 %copy-start.25 = (s32[25]{0:T(128)S(1)}, s32[25]{0:T(128)}, u32[]{:S(2)}) copy-start(s32[25]{0:T(128)} %param.29) | copy-start | bytes 304
  427.7 11.9 %all-to-all-start = ((s32[8,1,8]{2,1,0:T(1,128)}), s32[8,1,8]{2,1,0:T(1,128)S(1)}, u32[]{:S(2)}, u32[]{:S(2)}) async-start(s32[8,1,8]{2,1,0:T(1,128)} %bitcast.1), calls=%async_computation | async-start | bytes 8192 | tf_op jit(solution)/shard_map/all_to_all | solution.py:208
  439.6 14.8 %all-to-all-start.3 = ((bf16[8,8,112]{2,1,0:T(8,128)(2,1)}), bf16[8,8,112]{2,1,0:T(8,128)(2,1)S(1)}, u32[]{:S(2)}, u32[]{:S(2)}) async-start(bf16[8,8,112]{2,1,0:T(8,128)(2,1)} %bitcast.72), calls=%async_computation.3 | async-start | bytes 32768 | tf_op jit(solution)/shard_map/all_to_all | solution.py:201
  452.5 17.4 %copy-start.15 = (bf16[4,56,256]{2,1,0:T(8,128)(2,1)S(1)}, bf16[4,56,256]{2,1,0:T(8,128)(2,1)}, u32[]{:S(2)}) copy-start(bf16[4,56,256]{2,1,0:T(8,128)(2,1)} %param.31) | copy-start | bytes 344068
  453.3 33.8 %copy-start.18 = (bf16[4,20,256]{2,0,1:T(4,128)(2,1)S(1)}, bf16[4,20,256]{2,0,1:T(4,128)(2,1)}, u32[]{:S(2)}) copy-start(bf16[4,20,256]{2,0,1:T(4,128)(2,1)} %param.32) | copy-start | bytes 122884
  454.4 32.9 %copy-start.6 = (bf16[4,256,256]{2,1,0:T(8,128)(2,1)S(1)}, bf16[4,256,256]{2,1,0:T(8,128)(2,1)}, u32[]{:S(2)}) copy-start(bf16[4,256,256]{2,1,0:T(8,128)(2,1)} %param.33) | copy-start | bytes 1572868
  454.4 7.2 %all-to-all-start.1 = ((bf16[4,2,576]{2,1,0:T(2,128)(2,1)}), bf16[4,2,576]{2,1,0:T(2,128)(2,1)S(1)}, u32[]{:S(2)}, u32[]{:S(2)}) async-start(bf16[4,2,576]{2,1,0:T(2,128)(2,1)} %reshape.332), calls=%async_computation.1 | async-start | bytes 20480 | tf_op jit(solution)/shard_map/all_to_all | solution.py:184
  462.4 25.2 %copy-start.7 = (bf16[4,256,256]{2,1,0:T(8,128)(2,1)S(1)}, bf16[4,256,256]{2,1,0:T(8,128)(2,1)}, u32[]{:S(2)}) copy-start(bf16[4,256,256]{2,1,0:T(8,128)(2,1)} %param.34) | copy-start | bytes 1572868
  464.3 12.2 %all-to-all-start.2 = ((bf16[8,8,192]{2,1,0:T(8,128)(2,1)}), bf16[8,8,192]{2,1,0:T(8,128)(2,1)S(1)}, u32[]{:S(2)}, u32[]{:S(2)}) async-start(bf16[8,8,192]{2,1,0:T(8,128)(2,1)} %reshape.234), calls=%async_computation.2 | async-start | bytes 65536 | tf_op jit(solution)/shard_map/all_to_all | solution.py:194
  470.0 17.7 %copy-start.23 = (bf16[4,256,56]{1,2,0:T(8,128)(2,1)S(1)}, bf16[4,256,56]{1,2,0:T(8,128)(2,1)}, u32[]{:S(2)}) copy-start(bf16[4,256,56]{1,2,0:T(8,128)(2,1)} %param.35) | copy-start | bytes 344068
  495.4 10.0 %all-to-all-start.4 = ((bf16[8,8,192]{2,1,0:T(8,128)(2,1)}), bf16[8,8,192]{2,1,0:T(8,128)(2,1)S(1)}, u32[]{:S(2)}, u32[]{:S(2)}) async-start(bf16[8,8,192]{2,1,0:T(8,128)(2,1)} %copy.339), calls=%async_computation.4 | async-start | bytes 65536 | tf_op jit(solution)/shard_map/all_to_all | solution.py:273
  506.6 7.0 %all-to-all-start.5 = ((bf16[12,2,192]{2,1,0:T(2,128)(2,1)}), bf16[12,2,192]{2,1,0:T(2,128)(2,1)S(1)}, u32[]{:S(2)}, u32[]{:S(2)}) async-start(bf16[12,2,192]{2,1,0:T(2,128)(2,1)} %gather_fusion), calls=%async_computation.5 | async-start | bytes 24576 | tf_op jit(solution)/shard_map/all_to_all | solution.py:275
  (10 other events, 15.3 us)
Sparse Core Ops, SparseCore 0:
  13.4 20.1 all-gather.15
  98.5 27.6 reduce-scatter.12
  210.6 25.6 reduce-scatter.14
  315.7 25.7 reduce-scatter.16
  425.8 25.6 reduce-scatter.18
Sparse Core Ops, SparseCore 1:
  101.6 43.4 all-gather.23
  147.7 39.7 all-gather.25
  189.5 15.6 all-gather.17
  238.6 17.3 all-gather.19
  318.6 41.5 all-gather.27
  362.9 39.7 all-gather.29
  404.7 15.6 all-gather.21
